TPU v7x, 32 devices: a whole 2x2x4 slice. The times are simulated.
32 devices in a mesh: grid: 8 (over y, x, core), band: 4 (over z).
Axes of the slice: x: 2, y: 2, z: 4, core: 2. Of those that a mesh axis runs over, the one named last changes fastest.
Arguments:
- orbitals: bfloat16 [32, 64, 64, 128], P('band', 'grid'), may hold values from -6 to 6
- occupation: int32 [32], P('band'), may hold values from 1 to 2
- spin_of_band: int32 [32], P('band'), may hold values from 0 to 1
- ionic_charge: float32 [64, 64, 128], P('grid'), may hold values from 0.3 to 3
Outputs:
- potential: float32 [2, 64, 64, 128], P(None, 'grid')
- applied: bfloat16 [32, 64, 64, 128], P('band', 'grid')
All inputs are finite; a program needn't handle non-finite values.
Results may differ from a plain program's by a relative error of at most 0.001.
Values sent between devices are 32-bit elements; how exact they have to be, the bound alone decides.
A program may use at most 64 MiB of HBM per device.

v0:
```python
import math

import jax
import jax.numpy as jnp
from jax import lax
from jax.sharding import PartitionSpec as P

NZ = 64


spacing = 0.25
highest = lax.Precision.HIGHEST


def tables(count):
    index = jnp.arange(count, dtype=jnp.int32)
    product = index[:, None] * index[None, :] % count
    angle = 2.0 * math.pi * product.astype(jnp.float32) / count
    return (jnp.cos(angle), jnp.sin(angle))


def signed_sq(index, count):
    signed = jnp.where(index < count // 2, index, index - count).astype(jnp.float32)
    wave = 2.0 * math.pi * signed / (count * spacing)
    return wave * wave


def kernel_at(depth, row_index, rows, col_index, cols):
    g_sq = signed_sq(jnp.arange(depth, dtype=jnp.int32), depth)[:, None, None]
    g_sq = g_sq + signed_sq(row_index, rows)[None, :, None]
    g_sq = g_sq + signed_sq(col_index, cols)[None, None, :]
    return jnp.where(g_sq > 0, 4.0 * math.pi / jnp.where(g_sq > 0, g_sq, 1.0), 0.0)


def along(table, field, form):
    return jnp.einsum(form, table, field, precision=highest)


def forward_y(cos_y, sin_y, real_x, imag_x):
    form_y = "ky,zyx->zkx"
    real_y = along(cos_y, real_x, form_y) + along(sin_y, imag_x, form_y)
    imag_y = along(cos_y, imag_x, form_y) - along(sin_y, real_x, form_y)
    return (real_y, imag_y)


def inverse_y(cos_y, sin_y, real_k, imag_k):
    form_y = "ky,zyx->zkx"
    plane_real = along(cos_y, real_k, form_y) - along(sin_y, imag_k, form_y)
    plane_imag = along(cos_y, imag_k, form_y) + along(sin_y, real_k, form_y)
    return (plane_real, plane_imag)


def z_kernel(cos_z, sin_z, moved, kernel):
    form_z = "kz,zyx->kyx"
    real_z = along(cos_z, moved[0], form_z) + along(sin_z, moved[1], form_z)
    imag_z = along(cos_z, moved[1], form_z) - along(sin_z, moved[0], form_z)
    real_k = real_z * kernel
    imag_k = imag_z * kernel
    back_real = along(cos_z, real_k, form_z) - along(sin_z, imag_k, form_z)
    back_imag = along(cos_z, imag_k, form_z) + along(sin_z, real_k, form_z)
    return jnp.stack([back_real, back_imag])


def solve_hartree(net, depth):
    planes, rows, cols = net.shape
    cos_x, sin_x = tables(cols)
    cos_y, sin_y = tables(rows)
    cos_z, sin_z = tables(depth)
    local_rows = rows // lax.axis_size("grid")
    row_index = lax.axis_index("grid") * local_rows + jnp.arange(local_rows, dtype=jnp.int32)
    real_x = jnp.dot(net, cos_x, precision=highest)
    imag_x = -jnp.dot(net, sin_x, precision=highest)
    real_y, imag_y = forward_y(cos_y, sin_y, real_x, imag_x)
    moved = lax.all_to_all(
        jnp.stack([real_y, imag_y]), "grid", split_axis=2, concat_axis=1, tiled=True
    )
    kernel = kernel_at(depth, row_index, rows, jnp.arange(cols, dtype=jnp.int32), cols)
    back = z_kernel(cos_z, sin_z, moved, kernel)
    returned = lax.all_to_all(back, "grid", split_axis=1, concat_axis=2, tiled=True)
    plane_real, plane_imag = inverse_y(cos_y, sin_y, returned[0], returned[1])
    result = jnp.dot(plane_real, cos_x, precision=highest) - jnp.dot(
        plane_imag, sin_x, precision=highest
    )
    return result / (cols * rows * depth)


def local(orbitals, occupation, spin_of_band, ionic_charge):
    bands, planes, rows, cols = orbitals.shape
    total = bands * lax.axis_size("band")
    channels = jnp.arange(2, dtype=jnp.int32)
    weights = (
        jnp.where(
            spin_of_band[None, :] == channels[:, None], occupation[None, :].astype(jnp.float32), 0.0
        )
        / total
    )
    values = orbitals.astype(jnp.float32)
    squares = (values * values).reshape(bands, -1)
    partial_value = jnp.dot(weights, squares, precision=highest).reshape(2, planes, rows, cols)
    share = lax.psum_scatter(partial_value, "band", scatter_dimension=2, tiled=True)
    share_rows = share.shape[2]
    ion_share = lax.dynamic_slice_in_dim(
        ionic_charge, lax.axis_index("band") * share_rows, share_rows, 1
    )
    fields = jnp.concatenate(
        [-jnp.cbrt(6.0 / math.pi * share), (share[0] + share[1] - ion_share)[None]], 0
    )
    whole = lax.all_gather(fields, "band", axis=2, tiled=True)
    potential = solve_hartree(whole[2], NZ)[None] + whole[:2]
    pick = (spin_of_band[:, None] == channels[None, :]).astype(jnp.float32)
    chosen = jnp.dot(pick, potential.reshape(2, -1), precision=highest).reshape(
        bands, planes, rows, cols
    )
    applied = (chosen * values).astype(jnp.bfloat16)
    return (potential, applied)


def solution(mesh):
    return jax.shard_map(
        local,
        mesh=mesh,
        in_specs=(P("band", "grid", None, None), P("band"), P("band"), P("grid", None, None)),
        out_specs=(P(None, "grid", None, None), P("band", "grid", None, None)),
        check_vma=False,
    )
```

profile of v0, /device:TPU:0, one launch (start us, length us, event | category | flops | bytes accessed | tf_op | source)
XLA Modules:
  0.0 105.7 jit_solution(1825945070237419519)
XLA Ops:
  7.2 0.0 reduce-scatter.2.cloned.1.call-start
  7.2 0.7 convert_element_type.76
  7.9 3.5 %fusion.1 = f32[2,8,64,128]{3,0,2,1:T(2,128)S(1)} fusion(bf16[8,8,64,128]{3,2,1,0:T(8,128)(2,1)} %param.4, f32[8]{0:T(128)S(1)} %convert_element_type.76, s32[8]{0:T(128)} %param.6), kind=kOutput, calls=%fused_computation.3 | convolution fusion | flops 13631536 | bytes 1572928 | tf_op jit(solution)/shard_map/dot_general | solution.py:99
  11.3 1.1 %copy.29 = f32[2,8,64,128]{3,1,0,2:T(8,128)} copy(f32[2,8,64,128]{3,0,2,1:T(2,128)S(1)} %fusion.1) | data formatting | bytes 1048576 | tf_op jit(solution)/shard_map/dot_general | solution.py:99
  12.4 0.0 reduce-scatter.2.cloned.1.call-update
  12.5 24.7 %reduce-scatter.2.cloned.1.call-done = f32[2,8,16,128]{3,1,0,2:T(8,128)} async-done(((f32[2,8,64,128]{3,1,0,2:T(8,128)}), f32[2,8,16,128]{3,1,0,2:T(8,128)}) %reduce-scatter.2.cloned.1.call-update) | async-done | bytes 131088 | tf_op jit(solution)/shard_map/reduce_scatter | solution.py:100
  37.2 1.0 cbrt_negate_fusion
  38.2 0.9 fusion.34
  39.1 17.2 %all_gather.3 = f32[3,8,64,128]{3,2,1,0:T(8,128)S(1)} all-gather(f32[3,8,16,128]{3,2,1,0:T(8,128)S(1)} %pad_maximum_fusion.2), channel_id=1, replica_groups=mesh['grid'=8,'band'=4] {'band'}, dimensions={2}, use_global_device_ids=true | all-gather | bytes 983040 | tf_op jit(solution)/shard_map/all_gather | solution.py:108
  56.3 0.6 convolution_negate_fusion
  57.0 0.6 fusion.22
  57.6 0.5 fusion.64
  58.1 0.5 fusion.62
  58.6 0.5 fusion.12
  59.2 0.5 fusion.11
  59.8 1.1 %copy.33 = f32[2,8,64,128]{3,1,0,2:T(8,128)} copy(f32[2,8,64,128]{3,2,1,0:T(8,128)S(1)} %pad_maximum_fusion) | data formatting | bytes 1048576 | tf_op jit(solution)/shard_map/stack | solution.py:75
  60.9 3.6 %all-to-all-start = ((f32[2,8,64,128]{3,1,0,2:T(8,128)}), f32[2,8,64,128]{3,1,0,2:T(8,128)S(1)}, u32[]{:S(2)}, u32[]{:S(2)}) async-start(f32[2,8,64,128]{3,1,0,2:T(8,128)} %copy.33), calls=%async_computation.1 | async-start | bytes 1048576 | tf_op jit(solution)/shard_map/all_to_all | solution.py:74
  64.5 0.1 broadcast_add_fusion
  64.6 9.6 %all-to-all-done = f32[2,8,64,128]{3,1,0,2:T(8,128)S(1)} async-done(((f32[2,8,64,128]{3,1,0,2:T(8,128)}), f32[2,8,64,128]{3,1,0,2:T(8,128)S(1)}, u32[]{:S(2)}, u32[]{:S(2)}) %all-to-all-start) | async-done | bytes 524320 | tf_op jit(solution)/shard_map/all_to_all | solution.py:74
  74.3 0.5 fusion.24
  74.8 0.5 fusion.23
  75.3 0.5 fusion.9
  75.8 0.5 fusion.56
  76.3 0.5 fusion.10
  76.9 0.5 fusion.59
  77.4 0.5 fusion.7
  77.9 0.5 fusion.8
  78.5 0.3 copy.35
  78.8 12.1 %all_to_all.30 = f32[2,64,8,128]{3,2,0,1:T(8,128)S(1)} all-to-all(f32[2,64,8,128]{3,2,0,1:T(8,128)S(1)} %copy.35), channel_id=1, replica_groups=mesh['grid'=8,'band'=4] {'grid'}, dimensions={1} | all-to-all | bytes 1048576 | tf_op jit(solution)/shard_map/all_to_all | solution.py:79
  91.0 0.5 fusion.16
  91.5 0.5 fusion.20
  92.1 0.5 fusion.5
  92.6 0.5 fusion.6
  93.1 0.6 fusion.37
  93.8 0.6 fusion.4
  94.4 0.0 copy-start
  94.4 0.0 copy-start.2
  94.4 0.1 slice_add_fusion
  94.5 0.0 copy-start.1
  94.5 0.4 copy.68
  94.9 0.9 copy-done
  95.8 0.0 copy-done.2
  95.8 1.8 %fusion.3 = bf16[8,8,64,128]{3,0,2,1:T(8,128)(2,1)S(1)} fusion(f32[8,64,128,2]{2,3,1,0:T(2,128)S(1)} %bitcast.140, bf16[8,8,64,128]{3,2,1,0:T(8,128)(2,1)S(1)} %copy-done, s32[8]{0:T(128)S(1)} %copy-done.2), kind=kOutput, calls=%fused_computation.4 | convolution fusion | flops 14155792 | bytes 2621472 | tf_op jit(solution)/shard_map/dot_general | solution.py:111
  97.6 0.0 copy-done.1
  97.6 1.2 %copy.39 = bf16[8,8,64,128]{3,2,1,0:T(8,128)(2,1)} copy(bf16[8,8,64,128]{3,0,2,1:T(8,128)(2,1)S(1)} %fusion.3) | data formatting | bytes 2097152
  (9 shorter events, 0.2 us)
Async XLA Ops:
  7.2 30.0 %reduce-scatter.2.cloned.1.call-start = ((), (), s32[]{:S(2)}) async-start(), calls=%async_computation.3 | async-start | bytes 655360 | tf_op jit(solution)/shard_map/reduce_scatter | solution.py:100
  60.9 13.3 %all-to-all-start = ((f32[2,8,64,128]{3,1,0,2:T(8,128)}), f32[2,8,64,128]{3,1,0,2:T(8,128)S(1)}, u32[]{:S(2)}, u32[]{:S(2)}) async-start(f32[2,8,64,128]{3,1,0,2:T(8,128)} %copy.33), calls=%async_computation.1 | async-start | bytes 1048576 | tf_op jit(solution)/shard_map/all_to_all | solution.py:74
  94.4 1.4 %copy-start = (bf16[8,8,64,128]{3,2,1,0:T(8,128)(2,1)S(1)}, bf16[8,8,64,128]{3,2,1,0:T(8,128)(2,1)}, u32[]{:S(2)}) copy-start(bf16[8,8,64,128]{3,2,1,0:T(8,128)(2,1)} %param.4) | copy-start | bytes 3145732
  94.4 1.4 %copy-start.2 = (s32[8]{0:T(128)S(1)}, s32[8]{0:T(128)}, u32[]{:S(2)}) copy-start(s32[8]{0:T(128)} %param.6) | copy-start | bytes 100
  94.5 3.2 %copy-start.1 = (f32[2,8,64,128]{3,2,1,0:T(8,128)}, f32[2,8,64,128]{3,2,1,0:T(8,128)S(1)}, u32[]{:S(2)}) copy-start(f32[2,8,64,128]{3,2,1,0:T(8,128)S(1)} %slice_add_fusion) | copy-start | bytes 1572868
Sparse Core Ops, SparseCore 0:
  12.6 24.5 reduce-scatter.1
where the time goes:
time: 106 us
  waiting for transfers between devices  34.3 us (32%)
  blocking collectives  29.4 us (28%)
  matrix products  16 us (15%)
  between operations  14.3 us (13%)
  local copies, waits for them, and re-layouts  5.2 us (5%)
  starting transfers between devices  3.67 us (3%)
  other arithmetic  2.81 us (3%)
    reduce_scatter x1, waiting for transfers between devices, local(): lax.psum_scatter(partial_value, 'band', scatter_dimension=2, tiled=True)  24.7 us
    all_gather x1, blocking collectives, local(): whole = lax.all_gather(fields, 'band', axis=2, tiled=True)  17.2 us
    all_to_all x1, blocking collectives, solve_hartree(): lax.all_to_all(back, 'grid', split_axis=1, concat_axis=2, tiled=True)  12.1 us
    all_to_all x1, waiting for transfers between devices, solve_hartree(): lax.all_to_all(jnp.stack([real_y, imag_y]), 'grid', split_axis=2, concat_...  9.6 us
    dot_general x16, matrix products, along(): return jnp.einsum(form, table, field, precision=highest)  8.32 us
    all_to_all x1, starting transfers between devices, solve_hartree(): lax.all_to_all(jnp.stack([real_y, imag_y]), 'grid', split_axis=2, concat_...  3.63 us
    dot_general x1, matrix products, local(): jnp.dot(weights, squares, precision=highest).reshape(2, planes, rows, cols)  3.45 us
    unnamed x8, local copies, waits for them, and re-layouts  2.57 us
  transfers between devices with their start and end apart: 2, of which 2 were waited for; matrix products, arithmetic and copies ran while one was open for 0% of the time, Pallas kernels for 0%

commit v1 on v0

--- a/solution.py
+++ b/solution.py
@@ -1,12 +1,13 @@
+import functools
 import math
 
 import jax
 import jax.numpy as jnp
+import numpy as np
 from jax import lax
+from jax.experimental import pallas as pl
+from jax.experimental.pallas import tpu as pltpu
 from jax.sharding import PartitionSpec as P
-
-NZ = 64
-
 
 spacing = 0.25
 highest = lax.Precision.HIGHEST
@@ -84,7 +85,7 @@
     return result / (cols * rows * depth)
 
 
-def local(orbitals, occupation, spin_of_band, ionic_charge):
+def local(ng, orbitals, occupation, spin_of_band, ionic_charge):
     bands, planes, rows, cols = orbitals.shape
     total = bands * lax.axis_size("band")
     channels = jnp.arange(2, dtype=jnp.int32)
@@ -106,7 +107,7 @@
         [-jnp.cbrt(6.0 / math.pi * share), (share[0] + share[1] - ion_share)[None]], 0
     )
     whole = lax.all_gather(fields, "band", axis=2, tiled=True)
-    potential = solve_hartree(whole[2], NZ)[None] + whole[:2]
+    potential = solve_hartree(whole[2], planes * ng)[None] + whole[:2]
     pick = (spin_of_band[:, None] == channels[None, :]).astype(jnp.float32)
     chosen = jnp.dot(pick, potential.reshape(2, -1), precision=highest).reshape(
         bands, planes, rows, cols
@@ -114,10 +115,365 @@
     applied = (chosen * values).astype(jnp.bfloat16)
     return (potential, applied)
 
+MESH = pl.DeviceIdType.MESH
+f32 = jnp.float32
+bf16 = jnp.bfloat16
+
+
+def cas_table(count):
+    product = np.outer(np.arange(count), np.arange(count)) % count
+    angle = 2.0 * math.pi * product / count
+    return (np.cos(angle) + np.sin(angle)) / math.sqrt(count)
+
+
+def parts_of(table):
+    high = table.astype(np.float32).astype(bf16)
+    low = (table - high.astype(np.float64)).astype(np.float32).astype(bf16)
+    return high, low
+
+
+def right_table(count):
+    high, low = parts_of(cas_table(count))
+    return np.concatenate([high, high, low], 0)
+
+
+def left_table(count):
+    high, low = parts_of(cas_table(count))
+    return np.concatenate([high, low, high], 1)
+
+
+def two_parts(value):
+    high = value.astype(bf16)
+    low = (value - high.astype(f32)).astype(bf16)
+    return high, low
+
+
+def right_mul(value, table):
+    high, low = two_parts(value)
+    return jnp.dot(jnp.concatenate([high, low, high], 1), table, preferred_element_type=f32)
+
+
+def left_mul(table, value):
+    high, low = two_parts(value)
+    return jnp.dot(table, jnp.concatenate([high, high, low], 0), preferred_element_type=f32)
+
+
+def cube_root(value):
+    safe = jnp.where(value > 0, value, 1.0)
+    return jnp.where(value > 0, jnp.exp(jnp.log(safe) * (1.0 / 3.0)), 0.0)
+
+
+def wave_sq(index, count):
+    signed = jnp.where(index < count // 2, index, index - count).astype(f32)
+    wave = signed * (2.0 * math.pi / (count * spacing))
+    return wave * wave
+
+
+def field_kernel(
+    ng, nb, lag,
+    occ, spin, orb_hbm, ion_hbm, hx_hbm, hy_hbm, hz_hbm,
+    pot,
+    orb, ion, hx, hy, hz, part, near_in, near_out, far_in, far_out, ex,
+    y_out, z_in, z_out, y_in,
+    orb_sem, in_sem, near_s, near_r, far_s, far_r, fwd_s, fwd_r, back_s, back_r,
+):
+    bands, planes, rows, cols = orb.shape
+    depth = planes * ng
+    lines = rows // ng
+    g = lax.axis_index("grid")
+    i = lax.axis_index("band")
+    side = (2 * i) // nb
+    inner = jnp.logical_and(i > 0, i < nb - 1)
+    inward = i + 1 - 2 * side
+    outward = jnp.clip(i - 1 + 2 * side, 0, nb - 1)
+
+    barrier = pltpu.get_barrier_semaphore()
+    for k in range(1, ng):
+        pl.semaphore_signal(barrier, inc=1, device_id={"grid": lax.rem(g + k, ng)}, device_id_type=MESH)
+    pl.semaphore_signal(barrier, inc=1, device_id={"band": inward}, device_id_type=MESH)
+
+    @pl.when(inner)
+    def _():
+        pl.semaphore_signal(barrier, inc=1, device_id={"band": outward}, device_id_type=MESH)
+
+    loads = []
+    for p in range(planes):
+        copy = pltpu.make_async_copy(orb_hbm.at[:, p], orb.at[:, p], orb_sem.at[p])
+        copy.start()
+        loads.append(copy)
+    others = []
+    for k, (src, dst) in enumerate(((ion_hbm, ion), (hx_hbm, hx), (hy_hbm, hy), (hz_hbm, hz))):
+        copy = pltpu.make_async_copy(src, dst, in_sem.at[k])
+        copy.start()
+        others.append(copy)
+
+    scale = 1.0 / (bands * nb)
+    up = [occ[b].astype(f32) * spin[b].astype(f32) * scale for b in range(bands)]
+    down = [occ[b].astype(f32) * (1 - spin[b]).astype(f32) * scale for b in range(bands)]
+
+    def near_copy(p):
+        return pltpu.make_async_remote_copy(
+            src_ref=near_out.at[p], dst_ref=far_in.at[p],
+            send_sem=near_s.at[p], recv_sem=far_r.at[p],
+            device_id={"band": inward}, device_id_type=MESH,
+        )
+
+    def crossing(p):
+        return pltpu.make_async_remote_copy(
+            src_ref=near_out.at[p], dst_ref=near_in.at[p],
+            send_sem=near_s.at[p], recv_sem=near_r.at[p],
+            device_id={"band": inward}, device_id_type=MESH,
+        )
+
+    def far_copy(p):
+        return pltpu.make_async_remote_copy(
+            src_ref=far_out.at[p], dst_ref=far_in.at[p],
+            send_sem=far_s.at[p], recv_sem=far_r.at[p],
+            device_id={"band": outward}, device_id_type=MESH,
+        )
+
+    middle = jnp.where(side == 0, i + 1 == nb // 2, i == nb // 2)
+
+    def send_near(p):
+        @pl.when(middle)
+        def _():
+            near_copy(p).start()
+
+        @pl.when(jnp.logical_not(middle))
+        def _():
+            crossing(p).start()
+
+    def density(p):
+        loads[p].wait()
+        zero = one = None
+        for b in range(bands):
+            value = orb[b, p].astype(f32)
+            square = value * value
+            zero = down[b] * square if b == 0 else zero + down[b] * square
+            one = up[b] * square if b == 0 else one + up[b] * square
+        return zero, one
+
+    def near_step(p):
+        @pl.when(inner)
+        def _():
+            near_r_wait = crossing(p)
+            near_r_wait.wait_recv()
+            near_out[p] = part[p] + near_in[p]
+
+        @pl.when(inner)
+        def _():
+            send_near(p)
+
+    def fwd_copy(p, k):
+        target = lax.rem(g + k, ng)
+        return pltpu.make_async_remote_copy(
+            src_ref=y_out.at[target, pl.ds(p * lines, lines)],
+            dst_ref=z_in.at[pl.ds(pl.multiple_of((g * planes + p) * lines, lines), lines)],
+            send_sem=fwd_s.at[p, k], recv_sem=fwd_r.at[p, k],
+            device_id={"grid": target}, device_id_type=MESH,
+        )
+
+    def far_step(p):
+        far_copy(p).wait_recv()
+
+        @pl.when(inner)
+        def _():
+            far_out[p] = part[p] + far_in[p]
+            far_copy(p).start()
+
+        zero = near_out[p, 0] + far_in[p, 0]
+        one = near_out[p, 1] + far_in[p, 1]
+        net = zero + one - ion[p]
+        spectrum = left_mul(hy[...], right_mul(net, hx[...]))
+        for t in range(ng):
+            y_out[t, pl.ds(p * lines, lines)] = spectrum[t * lines:(t + 1) * lines]
+        for k in range(1, ng):
+            fwd_copy(p, k).start()
+        z_in[pl.ds(pl.multiple_of((g * planes + p) * lines, lines), lines)] = y_out[g, pl.ds(p * lines, lines)]
+        ex[0, p] = -cube_root(zero * (6.0 / math.pi))
+        ex[1, p] = -cube_root(one * (6.0 / math.pi))
+
+    for p in range(planes):
+        zero, one = density(p)
+        part[p, 0] = zero
+        part[p, 1] = one
+
+        @pl.when(jnp.logical_not(inner))
+        def _():
+            near_out[p, 0] = zero
+            near_out[p, 1] = one
+
+        if p == 0:
+            pl.semaphore_wait(barrier, ng + jnp.where(inner, 1, 0))
+
+        @pl.when(jnp.logical_not(inner))
+        def _():
+            send_near(p)
+
+    for copy in others:
+        copy.wait()
+    for step in range(planes + lag):
+        if step < planes:
+            near_step(step)
+        if step >= lag:
+            far_step(step - lag)
+
+    kz = lax.broadcasted_iota(jnp.int32, (depth, cols), 0)
+    kx = lax.broadcasted_iota(jnp.int32, (depth, cols), 1)
+    flat = wave_sq(kz, depth) + wave_sq(kx, cols)
+
+    def kernel_of(line):
+        total = flat + wave_sq(g * lines + line, rows)
+        return jnp.where(total > 0, 4.0 * math.pi / jnp.where(total > 0, total, 1.0), 0.0)
+
+    for p in range(planes):
+        for k in range(1, ng):
+            fwd_copy(p, k).wait_recv()
+
+    group = 2
+
+    def back_copy(start, k):
+        target = lax.rem(g + k, ng)
+        return pltpu.make_async_remote_copy(
+            src_ref=z_out.at[target, pl.ds(start * planes, group * planes)],
+            dst_ref=y_in.at[pl.ds(pl.multiple_of((g * lines + start) * planes, group * planes), group * planes)],
+            send_sem=back_s.at[start // group, k], recv_sem=back_r.at[start // group, k],
+            device_id={"grid": target}, device_id_type=MESH,
+        )
+
+    for start in range(0, lines, group):
+        picked = [z_in[pl.ds(start + t, depth, stride=lines), :] for t in range(group)]
+        weights = jnp.concatenate([kernel_of(start + t) for t in range(group)], 1)
+        waves = left_mul(hz[...], jnp.concatenate(picked, 1))
+        field = left_mul(hz[...], waves * weights)
+        for t in range(group):
+            for d in range(ng):
+                z_out[d, pl.ds((start + t) * planes, planes)] = field[
+                    d * planes:(d + 1) * planes, t * cols:(t + 1) * cols
+                ]
+        for k in range(1, ng):
+            back_copy(start, k).start()
+        y_in[pl.ds(pl.multiple_of((g * lines + start) * planes, group * planes), group * planes)] = z_out[
+            g, pl.ds(start * planes, group * planes)
+        ]
+
+    for start in range(0, lines, group):
+        for k in range(1, ng):
+            back_copy(start, k).wait_recv()
+
+    for p in range(0, planes, 2):
+        picked = [y_in[pl.ds(p + t, rows, stride=planes), :] for t in range(2)]
+        mixed = left_mul(hy[...], jnp.concatenate(picked, 1))
+        both = right_mul(jnp.concatenate([mixed[:, :cols], mixed[:, cols:]], 0), hx[...])
+        for t in range(2):
+            hartree = both[t * rows:(t + 1) * rows]
+            pot[0, p + t] = hartree + ex[0, p + t]
+            pot[1, p + t] = hartree + ex[1, p + t]
+
+    for p in range(planes):
+        near_copy(p).wait_send()
+
+        @pl.when(inner)
+        def _():
+            far_copy(p).wait_send()
+
+        for k in range(1, ng):
+            fwd_copy(p, k).wait_send()
+    for start in range(0, lines, group):
+        for k in range(1, ng):
+            back_copy(start, k).wait_send()
+
+
+def apply_kernel(spin, pot_in, orb, pot, out):
+    pot[...] = pot_in[...]
+    for b in range(orb.shape[0]):
+        chosen = jnp.where(spin[b] == 1, pot_in[1], pot_in[0])
+        out[b] = (chosen * orb[b].astype(f32)).astype(bf16)
+
+
+def fast(ng, nb, orbitals, occupation, spin_of_band, ionic_charge):
+    bands, planes, rows, cols = orbitals.shape
+    depth = planes * ng
+    lines = rows // ng
+    lag = 2
+    dma = pltpu.SemaphoreType.DMA
+    field = (planes, 2, rows, cols)
+    anywhere = pl.BlockSpec(memory_space=pl.ANY)
+    scalar = pl.BlockSpec(memory_space=pltpu.SMEM)
+    potential = pl.pallas_call(
+        functools.partial(field_kernel, ng, nb, lag),
+        name="fields",
+        out_shape=jax.ShapeDtypeStruct((2, planes, rows, cols), f32),
+        in_specs=[scalar, scalar] + [anywhere] * 5,
+        out_specs=pl.BlockSpec(memory_space=pltpu.VMEM),
+        scratch_shapes=[
+            pltpu.VMEM(orbitals.shape, bf16),
+            pltpu.VMEM((planes, rows, cols), f32),
+            pltpu.VMEM((3 * cols, cols), bf16),
+            pltpu.VMEM((rows, 3 * rows), bf16),
+            pltpu.VMEM((depth, 3 * depth), bf16),
+            pltpu.VMEM(field, f32),
+            pltpu.VMEM(field, f32),
+            pltpu.VMEM(field, f32),
+            pltpu.VMEM(field, f32),
+            pltpu.VMEM(field, f32),
+            pltpu.VMEM((2, planes, rows, cols), f32),
+            pltpu.VMEM((ng, planes * lines, cols), f32),
+            pltpu.VMEM((depth * lines, cols), f32),
+            pltpu.VMEM((ng, planes * lines, cols), f32),
+            pltpu.VMEM((rows * planes, cols), f32),
+            dma((planes,)),
+            dma((4,)),
+            dma((planes,)),
+            dma((planes,)),
+            dma((planes,)),
+            dma((planes,)),
+            dma((planes, ng)),
+            dma((planes, ng)),
+            dma((lines // 2, ng)),
+            dma((lines // 2, ng)),
+        ],
+        compiler_params=pltpu.CompilerParams(
+            collective_id=0, has_side_effects=True, vmem_limit_bytes=32 * 1024 * 1024
+        ),
+    )(
+        occupation, spin_of_band, orbitals, ionic_charge,
+        jnp.asarray(right_table(cols)), jnp.asarray(left_table(rows)), jnp.asarray(left_table(depth)),
+    )
+    step = 2
+    return pl.pallas_call(
+        apply_kernel,
+        name="apply",
+        grid=(planes // step,),
+        out_shape=(
+            jax.ShapeDtypeStruct(potential.shape, f32),
+            jax.ShapeDtypeStruct(orbitals.shape, bf16),
+        ),
+        in_specs=[
+            scalar,
+            pl.BlockSpec((2, step, rows, cols), lambda p: (0, p, 0, 0)),
+            pl.BlockSpec((bands, step, rows, cols), lambda p: (0, p, 0, 0)),
+        ],
+        out_specs=(
+            pl.BlockSpec((2, step, rows, cols), lambda p: (0, p, 0, 0)),
+            pl.BlockSpec((bands, step, rows, cols), lambda p: (0, p, 0, 0)),
+        ),
+    )(spin_of_band, potential, orbitals)
+
 
 def solution(mesh):
+    ng, nb = mesh.shape["grid"], mesh.shape["band"]
+
+    def body(orbitals, occupation, spin_of_band, ionic_charge):
+        bands, planes, rows, cols = orbitals.shape
+        lines = rows // ng
+        suits = planes % 8 == 0 and lines % 8 == 0 and rows % 16 == 0
+        if suits and cols % 128 == 0 and nb % 2 == 0 and ng > 1:
+            return fast(ng, nb, orbitals, occupation, spin_of_band, ionic_charge)
+        return local(ng, orbitals, occupation, spin_of_band, ionic_charge)
+
     return jax.shard_map(
-        local,
+        body,
         mesh=mesh,
         in_specs=(P("band", "grid", None, None), P("band"), P("band"), P("grid", None, None)),
         out_specs=(P(None, "grid", None, None), P("band", "grid", None, None)),

time: 106 us -> 48.6 us (0.46)
  Pallas kernels: 0 us -> 41.7 us
  waiting for transfers between devices: 34.3 us -> 0 us
  blocking collectives: 29.4 us -> 0 us
  matrix products: 16 us -> 0 us
  between operations: 14.3 us -> 0.66 us
  starting transfers between devices: 3.67 us -> 0 us
  other arithmetic: 2.81 us -> 0 us
    pallas_call x0 -> x2, Pallas kernels: none -> 41.7 us  [the longest x1 38 us: fast(): pl.pallas_call(functools.partial(field_kernel, ng, nb, lag), name='fields...]
    reduce_scatter x1 -> x0, waiting for transfers between devices: 24.7 us -> none  [local(): lax.psum_scatter(partial_value, 'band', scatter_dimension=2, tiled=True)]
    all_gather x1 -> x0, blocking collectives: 17.2 us -> none  [local(): whole = lax.all_gather(fields, 'band', axis=2, tiled=True)]
    dot_general x22 -> x0, matrix products: 16 us -> none  [the longest x16 8.32 us: along(): return jnp.einsum(form, table, field, precision=highest)]
    all_to_all x1 -> x0, blocking collectives: 12.1 us -> none  [solve_hartree(): lax.all_to_all(back, 'grid', split_axis=1, concat_axis=2, tiled=True)]
    all_to_all x1 -> x0, waiting for transfers between devices: 9.6 us -> none  [solve_hartree(): lax.all_to_all(jnp.stack([real_y, imag_y]), 'grid', split_axis=2, concat_...]
    all_to_all x1 -> x0, starting transfers between devices: 3.63 us -> none  [solve_hartree(): lax.all_to_all(jnp.stack([real_y, imag_y]), 'grid', split_axis=2, concat_...]
    unnamed x8 -> x14, local copies, waits for them, and re-layouts: 2.57 us -> 5.91 us
  transfers between devices with their start and end apart: 2 -> 0, of which waited for: 2 -> 0; matrix products, arithmetic and copies ran while one was open for 0% -> 0% of each run, Pallas kernels for 0% -> 0%
where the time goes in v1:
time: 48.6 us; the launch traced here: 48.3 us
  Pallas kernels  41.7 us (86%)
  local copies, waits for them, and re-layouts  5.91 us (12%)
  between operations  0.66 us (1%)
    pallas_call x1, Pallas kernels, fast(): pl.pallas_call(functools.partial(field_kernel, ng, nb, lag), name='fields...  38 us
    unnamed x14, local copies, waits for them, and re-layouts  5.91 us
    pallas_call x1, Pallas kernels, fast(): pl.pallas_call(apply_kernel, name='apply', grid=(planes // step,), out_sh...  3.73 us

profile of v1, /device:TPU:0, one launch (start us, length us, event | category | flops | bytes accessed | tf_op | source)
XLA Modules:
  0.0 48.3 jit_solution(13592020849534078040)
XLA Ops:
  0.6 0.0 copy-start
  0.6 1.2 %copy-done = bf16[8,8,64,128]{3,2,1,0:T(8,128)(2,1)S(1)} copy-done((bf16[8,8,64,128]{3,2,1,0:T(8,128)(2,1)S(1)}, bf16[8,8,64,128]{3,2,1,0:T(8,128)(2,1)}, u32[]{:S(2)}) %copy-start) | copy-done | bytes 1048600
  1.9 0.0 copy-start.2
  1.9 0.9 %copy-done.2 = f32[8,64,128]{2,1,0:T(8,128)S(1)} copy-done((f32[8,64,128]{2,1,0:T(8,128)S(1)}, f32[8,64,128]{2,1,0:T(8,128)}, u32[]{:S(2)}) %copy-start.2) | copy-done | bytes 262168
  2.8 0.0 copy-start.3
  2.8 0.8 %copy-done.3 = bf16[64,192]{1,0:T(8,128)(2,1)S(1)} copy-done((bf16[64,192]{1,0:T(8,128)(2,1)S(1)}, bf16[64,192]{1,0:T(8,128)(2,1)}, u32[]{:S(2)}) %copy-start.3) | copy-done | bytes 24600
  3.6 0.0 copy-start.4
  3.6 0.9 %copy-done.4 = bf16[384,128]{1,0:T(8,128)(2,1)S(1)} copy-done((bf16[384,128]{1,0:T(8,128)(2,1)S(1)}, bf16[384,128]{1,0:T(8,128)(2,1)}, u32[]{:S(2)}) %copy-start.4) | copy-done | bytes 98328
  4.5 0.0 copy-start.5
  4.5 0.7 %copy-done.5 = s32[8]{0:T(128)S(1)} copy-done((s32[8]{0:T(128)S(1)}, s32[8]{0:T(128)}, u32[]{:S(2)}) %copy-start.5) | copy-done | bytes 56
  5.1 0.0 copy-start.6
  5.1 0.7 %copy-done.6 = s32[8]{0:T(128)S(1)} copy-done((s32[8]{0:T(128)S(1)}, s32[8]{0:T(128)}, u32[]{:S(2)}) %copy-start.6) | copy-done | bytes 56
  5.8 38.0 %fields.1.pot_in = f32[2,8,64,128]{3,2,1,0:T(8,128)S(1)} custom-call(s32[8]{0:T(128)S(1)} %copy-done.6, s32[8]{0:T(128)S(1)} %copy-done.5, bf16[8,8,64,128]{3,2,1,0:T(8,128)(2,1)S(1)} %copy-done, f32[8,64,128]{2,1,0:T(8,128)S(1)} %copy-done.2, bf16[384,128]{1,0:T(8,128)(2,1)S(1)} %copy-done.4, bf16[64,192]{1,0:T(8,128)(2,1)S(1)} %copy-done.3, ...), custom_call_target="tpu_custom_call" | custom-call | tf_op jit(solution)/shard_map/fields/pallas_call | solution.py:403
  43.7 0.0 copy-start.1
  43.7 0.8 %copy-done.1 = f32[2,8,64,128]{3,2,1,0:T(8,128)} copy-done((f32[2,8,64,128]{3,2,1,0:T(8,128)}, f32[2,8,64,128]{3,2,1,0:T(8,128)S(1)}, u32[]{:S(2)}) %copy-start.1) | copy-done | bytes 524312
  44.5 3.7 %apply.1 = (f32[2,8,64,128]{3,2,1,0:T(8,128)}, bf16[8,8,64,128]{3,2,1,0:T(8,128)(2,1)}) custom-call(s32[8]{0:T(128)} %spin.3, f32[2,8,64,128]{3,2,1,0:T(8,128)} %copy-done.1, bf16[8,8,64,128]{3,2,1,0:T(8,128)(2,1)} %orb.1), custom_call_target="tpu_custom_call" | custom-call | tf_op jit(solution)/shard_map/apply/pallas_call | solution.py:444
Async XLA Ops:
  0.6 1.2 %copy-start = (bf16[8,8,64,128]{3,2,1,0:T(8,128)(2,1)S(1)}, bf16[8,8,64,128]{3,2,1,0:T(8,128)(2,1)}, u32[]{:S(2)}) copy-start(bf16[8,8,64,128]{3,2,1,0:T(8,128)(2,1)} %orb.1) | copy-start | bytes 3145732
  1.9 0.9 %copy-start.2 = (f32[8,64,128]{2,1,0:T(8,128)S(1)}, f32[8,64,128]{2,1,0:T(8,128)}, u32[]{:S(2)}) copy-start(f32[8,64,128]{2,1,0:T(8,128)} %ion_hbm.1) | copy-start | bytes 786436
  2.8 0.8 %copy-start.3 = (bf16[64,192]{1,0:T(8,128)(2,1)S(1)}, bf16[64,192]{1,0:T(8,128)(2,1)}, u32[]{:S(2)}) copy-start(bf16[64,192]{1,0:T(8,128)(2,1)} %constant.5.clone.hy_hbm.hz_hbm) | copy-start | bytes 73732
  3.6 0.9 %copy-start.4 = (bf16[384,128]{1,0:T(8,128)(2,1)S(1)}, bf16[384,128]{1,0:T(8,128)(2,1)}, u32[]{:S(2)}) copy-start(bf16[384,128]{1,0:T(8,128)(2,1)} %constant.4.clone.hx_hbm) | copy-start | bytes 294916
  4.5 0.7 %copy-start.5 = (s32[8]{0:T(128)S(1)}, s32[8]{0:T(128)}, u32[]{:S(2)}) copy-start(s32[8]{0:T(128)} %spin.3) | copy-start | bytes 100
  5.1 0.7 %copy-start.6 = (s32[8]{0:T(128)S(1)}, s32[8]{0:T(128)}, u32[]{:S(2)}) copy-start(s32[8]{0:T(128)} %occ.1) | copy-start | bytes 100
  43.7 0.8 %copy-start.1 = (f32[2,8,64,128]{3,2,1,0:T(8,128)}, f32[2,8,64,128]{3,2,1,0:T(8,128)S(1)}, u32[]{:S(2)}) copy-start(f32[2,8,64,128]{3,2,1,0:T(8,128)S(1)} %fields.1.pot_in) | copy-start | bytes 1572868

commit v2 on v1

--- a/solution.py
+++ b/solution.py
@@ -171,21 +171,26 @@
 
 def field_kernel(
     ng, nb, lag,
-    occ, spin, orb_hbm, ion_hbm, hx_hbm, hy_hbm, hz_hbm,
-    pot,
-    orb, ion, hx, hy, hz, part, near_in, near_out, far_in, far_out, ex,
+    occ_hbm, spin_hbm, orb_hbm, ion_hbm, hx_hbm, hy_hbm, hz_hbm,
+    pot, applied,
+    occ, spin, orb, ion, hx, hy, hz, ex,
+    part_a, near_in_a, near_out_a, far_in_a, far_out_a,
+    part_b, near_in_b, near_out_b, far_in_b, far_out_b,
     y_out, z_in, z_out, y_in,
     orb_sem, in_sem, near_s, near_r, far_s, far_r, fwd_s, fwd_r, back_s, back_r,
 ):
     bands, planes, rows, cols = orb.shape
     depth = planes * ng
     lines = rows // ng
+    group = 2
     g = lax.axis_index("grid")
     i = lax.axis_index("band")
     side = (2 * i) // nb
     inner = jnp.logical_and(i > 0, i < nb - 1)
+    outer = jnp.logical_not(inner)
     inward = i + 1 - 2 * side
     outward = jnp.clip(i - 1 + 2 * side, 0, nb - 1)
+    middle = jnp.where(side == 0, i + 1 == nb // 2, i == nb // 2)
 
     barrier = pltpu.get_barrier_semaphore()
     for k in range(1, ng):
@@ -196,141 +201,71 @@
     def _():
         pl.semaphore_signal(barrier, inc=1, device_id={"band": outward}, device_id_type=MESH)
 
-    loads = []
-    for p in range(planes):
-        copy = pltpu.make_async_copy(orb_hbm.at[:, p], orb.at[:, p], orb_sem.at[p])
+    moves = [(occ_hbm, occ), (spin_hbm, spin)]
+    moves += [(ion_hbm, ion), (hx_hbm, hx), (hy_hbm, hy), (hz_hbm, hz)]
+    others = [pltpu.make_async_copy(src, dst, in_sem.at[k]) for k, (src, dst) in enumerate(moves)]
+    loads = [pltpu.make_async_copy(orb_hbm.at[:, p], orb.at[:, p], orb_sem.at[p]) for p in range(planes)]
+    for copy in others[:2] + loads + others[2:]:
         copy.start()
-        loads.append(copy)
-    others = []
-    for k, (src, dst) in enumerate(((ion_hbm, ion), (hx_hbm, hx), (hy_hbm, hy), (hz_hbm, hz))):
-        copy = pltpu.make_async_copy(src, dst, in_sem.at[k])
-        copy.start()
-        others.append(copy)
+    for copy in others[:2]:
+        copy.wait()
 
     scale = 1.0 / (bands * nb)
-    up = [occ[b].astype(f32) * spin[b].astype(f32) * scale for b in range(bands)]
-    down = [occ[b].astype(f32) * (1 - spin[b]).astype(f32) * scale for b in range(bands)]
-
-    def near_copy(p):
+    share = [spin[b].astype(f32) for b in range(bands)]
+    up = [occ[b].astype(f32) * share[b] * scale for b in range(bands)]
+    down = [occ[b].astype(f32) * (1.0 - share[b]) * scale for b in range(bands)]
+
+    chain_a = (0, part_a, near_in_a, near_out_a, far_in_a, far_out_a)
+    chain_b = (1, part_b, near_in_b, near_out_b, far_in_b, far_out_b)
+
+    def inward_copy(chain, p, landing):
+        n = chain[0]
         return pltpu.make_async_remote_copy(
-            src_ref=near_out.at[p], dst_ref=far_in.at[p],
-            send_sem=near_s.at[p], recv_sem=far_r.at[p],
+            src_ref=chain[3].at[p], dst_ref=(chain[4] if landing else chain[2]).at[p],
+            send_sem=near_s.at[n, p], recv_sem=(far_r if landing else near_r).at[n, p],
             device_id={"band": inward}, device_id_type=MESH,
         )
 
-    def crossing(p):
+    def far_copy(chain, p):
+        n = chain[0]
         return pltpu.make_async_remote_copy(
-            src_ref=near_out.at[p], dst_ref=near_in.at[p],
-            send_sem=near_s.at[p], recv_sem=near_r.at[p],
-            device_id={"band": inward}, device_id_type=MESH,
-        )
-
-    def far_copy(p):
-        return pltpu.make_async_remote_copy(
-            src_ref=far_out.at[p], dst_ref=far_in.at[p],
-            send_sem=far_s.at[p], recv_sem=far_r.at[p],
+            src_ref=chain[5].at[p], dst_ref=chain[4].at[p],
+            send_sem=far_s.at[n, p], recv_sem=far_r.at[n, p],
             device_id={"band": outward}, device_id_type=MESH,
         )
 
-    middle = jnp.where(side == 0, i + 1 == nb // 2, i == nb // 2)
-
-    def send_near(p):
+    def send_near(chain, p):
         @pl.when(middle)
         def _():
-            near_copy(p).start()
+            inward_copy(chain, p, True).start()
 
         @pl.when(jnp.logical_not(middle))
         def _():
-            crossing(p).start()
-
-    def density(p):
-        loads[p].wait()
-        zero = one = None
-        for b in range(bands):
-            value = orb[b, p].astype(f32)
-            square = value * value
-            zero = down[b] * square if b == 0 else zero + down[b] * square
-            one = up[b] * square if b == 0 else one + up[b] * square
-        return zero, one
-
-    def near_step(p):
+            inward_copy(chain, p, False).start()
+
+    def near_step(chain, p):
         @pl.when(inner)
         def _():
-            near_r_wait = crossing(p)
-            near_r_wait.wait_recv()
-            near_out[p] = part[p] + near_in[p]
+            inward_copy(chain, p, False).wait_recv()
+            chain[3][p] = chain[1][p] + chain[2][p]
+            send_near(chain, p)
+
+    def far_step(chain, p):
+        far_copy(chain, p).wait_recv()
 
         @pl.when(inner)
         def _():
-            send_near(p)
+            chain[5][p] = chain[1][p] + chain[4][p]
+            far_copy(chain, p).start()
 
     def fwd_copy(p, k):
         target = lax.rem(g + k, ng)
         return pltpu.make_async_remote_copy(
-            src_ref=y_out.at[target, pl.ds(p * lines, lines)],
-            dst_ref=z_in.at[pl.ds(pl.multiple_of((g * planes + p) * lines, lines), lines)],
-            send_sem=fwd_s.at[p, k], recv_sem=fwd_r.at[p, k],
+            src_ref=y_out.at[target, pl.ds(p * lines, group * lines)],
+            dst_ref=z_in.at[pl.ds(pl.multiple_of((g * planes + p) * lines, group * lines), group * lines)],
+            send_sem=fwd_s.at[p // group, k], recv_sem=fwd_r.at[p // group, k],
             device_id={"grid": target}, device_id_type=MESH,
         )
-
-    def far_step(p):
-        far_copy(p).wait_recv()
-
-        @pl.when(inner)
-        def _():
-            far_out[p] = part[p] + far_in[p]
-            far_copy(p).start()
-
-        zero = near_out[p, 0] + far_in[p, 0]
-        one = near_out[p, 1] + far_in[p, 1]
-        net = zero + one - ion[p]
-        spectrum = left_mul(hy[...], right_mul(net, hx[...]))
-        for t in range(ng):
-            y_out[t, pl.ds(p * lines, lines)] = spectrum[t * lines:(t + 1) * lines]
-        for k in range(1, ng):
-            fwd_copy(p, k).start()
-        z_in[pl.ds(pl.multiple_of((g * planes + p) * lines, lines), lines)] = y_out[g, pl.ds(p * lines, lines)]
-        ex[0, p] = -cube_root(zero * (6.0 / math.pi))
-        ex[1, p] = -cube_root(one * (6.0 / math.pi))
-
-    for p in range(planes):
-        zero, one = density(p)
-        part[p, 0] = zero
-        part[p, 1] = one
-
-        @pl.when(jnp.logical_not(inner))
-        def _():
-            near_out[p, 0] = zero
-            near_out[p, 1] = one
-
-        if p == 0:
-            pl.semaphore_wait(barrier, ng + jnp.where(inner, 1, 0))
-
-        @pl.when(jnp.logical_not(inner))
-        def _():
-            send_near(p)
-
-    for copy in others:
-        copy.wait()
-    for step in range(planes + lag):
-        if step < planes:
-            near_step(step)
-        if step >= lag:
-            far_step(step - lag)
-
-    kz = lax.broadcasted_iota(jnp.int32, (depth, cols), 0)
-    kx = lax.broadcasted_iota(jnp.int32, (depth, cols), 1)
-    flat = wave_sq(kz, depth) + wave_sq(kx, cols)
-
-    def kernel_of(line):
-        total = flat + wave_sq(g * lines + line, rows)
-        return jnp.where(total > 0, 4.0 * math.pi / jnp.where(total > 0, total, 1.0), 0.0)
-
-    for p in range(planes):
-        for k in range(1, ng):
-            fwd_copy(p, k).wait_recv()
-
-    group = 2
 
     def back_copy(start, k):
         target = lax.rem(g + k, ng)
@@ -341,6 +276,95 @@
             device_id={"grid": target}, device_id_type=MESH,
         )
 
+    def forward(p):
+        net = jnp.concatenate([near_out_a[q] + far_in_a[q] - ion[q] for q in (p, p + 1)], 0)
+        mixed = right_mul(net, hx[...])
+        spectrum = left_mul(hy[...], jnp.concatenate([mixed[:rows], mixed[rows:]], 1))
+        for q in range(group):
+            for t in range(ng):
+                y_out[t, pl.ds((p + q) * lines, lines)] = spectrum[
+                    t * lines:(t + 1) * lines, q * cols:(q + 1) * cols
+                ]
+        for k in range(1, ng):
+            fwd_copy(p, k).start()
+        z_in[pl.ds(pl.multiple_of((g * planes + p) * lines, group * lines), group * lines)] = y_out[
+            g, pl.ds(p * lines, group * lines)
+        ]
+
+    def exchange(p):
+        ex[p] = -cube_root((near_out_b[p] + far_in_b[p]) * (6.0 / math.pi))
+
+    def finish(p):
+        zero = pot[0, p] + ex[p, 0]
+        one = pot[1, p] + ex[p, 1]
+        pot[0, p] = zero
+        pot[1, p] = one
+        for b in range(bands):
+            chosen = zero * (1.0 - share[b]) + one * share[b]
+            applied[b, p] = (chosen * orb[b, p].astype(f32)).astype(bf16)
+
+    for p in range(planes):
+        loads[p].wait()
+        zero = one = None
+        for b in range(bands):
+            value = orb[b, p].astype(f32)
+            square = value * value
+            zero = down[b] * square if b == 0 else zero + down[b] * square
+            one = up[b] * square if b == 0 else one + up[b] * square
+        both = zero + one
+
+        @pl.when(inner)
+        def _():
+            part_a[p] = both
+            part_b[p, 0] = zero
+            part_b[p, 1] = one
+
+        @pl.when(outer)
+        def _():
+            near_out_a[p] = both
+            near_out_b[p, 0] = zero
+            near_out_b[p, 1] = one
+
+        if p == 0:
+            pl.semaphore_wait(barrier, ng + jnp.where(inner, 1, 0))
+
+        @pl.when(outer)
+        def _():
+            send_near(chain_a, p)
+
+    @pl.when(outer)
+    def _():
+        for p in range(planes):
+            send_near(chain_b, p)
+
+    for copy in others[2:]:
+        copy.wait()
+    for step in range(planes + lag):
+        if step < planes:
+            near_step(chain_a, step)
+        if step == planes + lag - 1:
+            near_step(chain_b, 0)
+        p = step - lag
+        if p >= 0:
+            far_step(chain_a, p)
+            if p % group == group - 1:
+                forward(p - group + 1)
+
+    near_step(chain_b, 1)
+    near_step(chain_b, 2)
+    far_step(chain_b, 0)
+
+    kz = lax.broadcasted_iota(jnp.int32, (depth, cols), 0)
+    kx = lax.broadcasted_iota(jnp.int32, (depth, cols), 1)
+    flat = wave_sq(kz, depth) + wave_sq(kx, cols)
+
+    def kernel_of(line):
+        total = flat + wave_sq(g * lines + line, rows)
+        return jnp.where(total > 0, 4.0 * math.pi / jnp.where(total > 0, total, 1.0), 0.0)
+
+    for p in range(0, planes, group):
+        for k in range(1, ng):
+            fwd_copy(p, k).wait_recv()
     for start in range(0, lines, group):
         picked = [z_in[pl.ds(start + t, depth, stride=lines), :] for t in range(group)]
         weights = jnp.concatenate([kernel_of(start + t) for t in range(group)], 1)
@@ -357,26 +381,43 @@
             g, pl.ds(start * planes, group * planes)
         ]
 
+    exchange(0)
+    for step in range(3, planes):
+        near_step(chain_b, step)
+        far_step(chain_b, step - 2)
+        exchange(step - 2)
+
     for start in range(0, lines, group):
         for k in range(1, ng):
             back_copy(start, k).wait_recv()
-
-    for p in range(0, planes, 2):
-        picked = [y_in[pl.ds(p + t, rows, stride=planes), :] for t in range(2)]
+    for p in range(0, planes, group):
+        picked = [y_in[pl.ds(p + t, rows, stride=planes), :] for t in range(group)]
         mixed = left_mul(hy[...], jnp.concatenate(picked, 1))
         both = right_mul(jnp.concatenate([mixed[:, :cols], mixed[:, cols:]], 0), hx[...])
-        for t in range(2):
+        for t in range(group):
             hartree = both[t * rows:(t + 1) * rows]
-            pot[0, p + t] = hartree + ex[0, p + t]
-            pot[1, p + t] = hartree + ex[1, p + t]
+            pot[0, p + t] = hartree
+            pot[1, p + t] = hartree
+    far_step(chain_b, planes - 2)
+    for p in range(planes - 2):
+        finish(p)
+    exchange(planes - 2)
+    finish(planes - 2)
+    far_step(chain_b, planes - 1)
+    exchange(planes - 1)
+    finish(planes - 1)
 
     for p in range(planes):
-        near_copy(p).wait_send()
-
-        @pl.when(inner)
-        def _():
-            far_copy(p).wait_send()
-
+        for chain in (chain_a, chain_b):
+            inward_copy(chain, p, False).wait_send()
+
+    @pl.when(inner)
+    def _():
+        for p in range(planes):
+            for chain in (chain_a, chain_b):
+                far_copy(chain, p).wait_send()
+
+    for p in range(0, planes, group):
         for k in range(1, ng):
             fwd_copy(p, k).wait_send()
     for start in range(0, lines, group):
@@ -384,52 +425,48 @@
             back_copy(start, k).wait_send()
 
 
-def apply_kernel(spin, pot_in, orb, pot, out):
-    pot[...] = pot_in[...]
-    for b in range(orb.shape[0]):
-        chosen = jnp.where(spin[b] == 1, pot_in[1], pot_in[0])
-        out[b] = (chosen * orb[b].astype(f32)).astype(bf16)
-
-
 def fast(ng, nb, orbitals, occupation, spin_of_band, ionic_charge):
     bands, planes, rows, cols = orbitals.shape
     depth = planes * ng
     lines = rows // ng
-    lag = 2
+    lag = 3
     dma = pltpu.SemaphoreType.DMA
-    field = (planes, 2, rows, cols)
-    anywhere = pl.BlockSpec(memory_space=pl.ANY)
-    scalar = pl.BlockSpec(memory_space=pltpu.SMEM)
-    potential = pl.pallas_call(
+    one = (planes, rows, cols)
+    two = (planes, 2, rows, cols)
+    return pl.pallas_call(
         functools.partial(field_kernel, ng, nb, lag),
         name="fields",
-        out_shape=jax.ShapeDtypeStruct((2, planes, rows, cols), f32),
-        in_specs=[scalar, scalar] + [anywhere] * 5,
-        out_specs=pl.BlockSpec(memory_space=pltpu.VMEM),
+        out_shape=(
+            jax.ShapeDtypeStruct((2, planes, rows, cols), f32),
+            jax.ShapeDtypeStruct(orbitals.shape, bf16),
+        ),
+        in_specs=[pl.BlockSpec(memory_space=pltpu.HBM)] * 7,
+        out_specs=(pl.BlockSpec(memory_space=pltpu.VMEM), pl.BlockSpec(memory_space=pltpu.VMEM)),
         scratch_shapes=[
+            pltpu.SMEM((bands,), jnp.int32),
+            pltpu.SMEM((bands,), jnp.int32),
             pltpu.VMEM(orbitals.shape, bf16),
-            pltpu.VMEM((planes, rows, cols), f32),
+            pltpu.VMEM(one, f32),
             pltpu.VMEM((3 * cols, cols), bf16),
             pltpu.VMEM((rows, 3 * rows), bf16),
             pltpu.VMEM((depth, 3 * depth), bf16),
-            pltpu.VMEM(field, f32),
-            pltpu.VMEM(field, f32),
-            pltpu.VMEM(field, f32),
-            pltpu.VMEM(field, f32),
-            pltpu.VMEM(field, f32),
-            pltpu.VMEM((2, planes, rows, cols), f32),
+            pltpu.VMEM(two, f32),
+        ]
+        + [pltpu.VMEM(one, f32)] * 5
+        + [pltpu.VMEM(two, f32)] * 5
+        + [
             pltpu.VMEM((ng, planes * lines, cols), f32),
             pltpu.VMEM((depth * lines, cols), f32),
             pltpu.VMEM((ng, planes * lines, cols), f32),
             pltpu.VMEM((rows * planes, cols), f32),
             dma((planes,)),
-            dma((4,)),
-            dma((planes,)),
-            dma((planes,)),
-            dma((planes,)),
-            dma((planes,)),
-            dma((planes, ng)),
-            dma((planes, ng)),
+            dma((6,)),
+            dma((2, planes)),
+            dma((2, planes)),
+            dma((2, planes)),
+            dma((2, planes)),
+            dma((planes // 2, ng)),
+            dma((planes // 2, ng)),
             dma((lines // 2, ng)),
             dma((lines // 2, ng)),
         ],
@@ -437,28 +474,10 @@
             collective_id=0, has_side_effects=True, vmem_limit_bytes=32 * 1024 * 1024
         ),
     )(
+        *(pltpu.with_memory_space_constraint(x, pltpu.HBM) for x in (
         occupation, spin_of_band, orbitals, ionic_charge,
         jnp.asarray(right_table(cols)), jnp.asarray(left_table(rows)), jnp.asarray(left_table(depth)),
-    )
-    step = 2
-    return pl.pallas_call(
-        apply_kernel,
-        name="apply",
-        grid=(planes // step,),
-        out_shape=(
-            jax.ShapeDtypeStruct(potential.shape, f32),
-            jax.ShapeDtypeStruct(orbitals.shape, bf16),
-        ),
-        in_specs=[
-            scalar,
-            pl.BlockSpec((2, step, rows, cols), lambda p: (0, p, 0, 0)),
-            pl.BlockSpec((bands, step, rows, cols), lambda p: (0, p, 0, 0)),
-        ],
-        out_specs=(
-            pl.BlockSpec((2, step, rows, cols), lambda p: (0, p, 0, 0)),
-            pl.BlockSpec((bands, step, rows, cols), lambda p: (0, p, 0, 0)),
-        ),
-    )(spin_of_band, potential, orbitals)
+    )))
 
 
 def solution(mesh):

time: 48.6 us -> 39.2 us (0.81)
  Pallas kernels: 41.7 us -> 36.7 us
  local copies, waits for them, and re-layouts: 5.91 us -> 1.77 us
    unnamed x14 -> x2, local copies, waits for them, and re-layouts: 5.91 us -> 1.77 us
    pallas_call x1 -> x0, Pallas kernels: 3.73 us -> none  [fast(): pl.pallas_call(apply_kernel, name='apply', grid=(planes // step,), out_sh...]
    pallas_call x1, Pallas kernels: 38 us -> 36.7 us  [fast(): pl.pallas_call(functools.partial(field_kernel, ng, nb, lag), name='fields...]
where the time goes in v2:
time: 39.2 us; the launch traced here: 39.1 us
  Pallas kernels  36.7 us (94%)
  local copies, waits for them, and re-layouts  1.77 us (5%)
  between operations  0.64 us (2%)
    pallas_call x1, Pallas kernels, fast(): pl.pallas_call(functools.partial(field_kernel, ng, nb, lag), name='fields...  36.7 us
    unnamed x2, local copies, waits for them, and re-layouts  1.77 us

profile of v2, /device:TPU:0, one launch (start us, length us, event | category | flops | bytes accessed | tf_op | source)
XLA Modules:
  0.0 39.1 jit_solution(17747759824413156024)
XLA Ops:
  0.6 36.7 %fields.1 = (f32[2,8,64,128]{3,2,1,0:T(8,128)S(1)}, bf16[8,8,64,128]{3,2,1,0:T(8,128)(2,1)S(1)}) custom-call(s32[8]{0:T(128)} %occ_hbm.1, s32[8]{0:T(128)} %spin_hbm.1, bf16[8,8,64,128]{3,2,1,0:T(8,128)(2,1)} %orb_hbm.1, f32[8,64,128]{2,1,0:T(8,128)} %ion_hbm.1, bf16[384,128]{1,0:T(8,128)(2,1)} %constant.4.clone.hx_hbm, ...), custom_call_target="tpu_custom_call" | custom-call | tf_op jit(solution)/shard_map/fields/pallas_call | solution.py:436
  37.3 0.8 %copy.11 = f32[2,8,64,128]{3,2,1,0:T(8,128)} copy(f32[2,8,64,128]{3,2,1,0:T(8,128)S(1)} %get-tuple-element.4) | data formatting | bytes 1048576
  38.1 1.0 %copy.12 = bf16[8,8,64,128]{3,2,1,0:T(8,128)(2,1)} copy(bf16[8,8,64,128]{3,2,1,0:T(8,128)(2,1)S(1)} %get-tuple-element.5) | data formatting | bytes 2097152

commit v3 on v2

--- a/solution.py
+++ b/solution.py
@@ -170,7 +170,7 @@
 
 
 def field_kernel(
-    ng, nb, lag,
+    ng, nb, lag, delay,
     occ_hbm, spin_hbm, orb_hbm, ion_hbm, hx_hbm, hy_hbm, hz_hbm,
     pot, applied,
     occ, spin, orb, ion, hx, hy, hz, ex,
@@ -350,8 +350,8 @@
             if p % group == group - 1:
                 forward(p - group + 1)
 
-    near_step(chain_b, 1)
-    near_step(chain_b, 2)
+    for p in range(1, delay + 1):
+        near_step(chain_b, p)
     far_step(chain_b, 0)
 
     kz = lax.broadcasted_iota(jnp.int32, (depth, cols), 0)
@@ -382,10 +382,10 @@
         ]
 
     exchange(0)
-    for step in range(3, planes):
+    for step in range(delay + 1, planes):
         near_step(chain_b, step)
-        far_step(chain_b, step - 2)
-        exchange(step - 2)
+        far_step(chain_b, step - delay)
+        exchange(step - delay)
 
     for start in range(0, lines, group):
         for k in range(1, ng):
@@ -398,14 +398,13 @@
             hartree = both[t * rows:(t + 1) * rows]
             pot[0, p + t] = hartree
             pot[1, p + t] = hartree
-    far_step(chain_b, planes - 2)
-    for p in range(planes - 2):
+    for p in range(planes - delay, planes):
+        far_step(chain_b, p)
+        if p == planes - delay:
+            for q in range(p):
+                finish(q)
+        exchange(p)
         finish(p)
-    exchange(planes - 2)
-    finish(planes - 2)
-    far_step(chain_b, planes - 1)
-    exchange(planes - 1)
-    finish(planes - 1)
 
     for p in range(planes):
         for chain in (chain_a, chain_b):
@@ -429,12 +428,12 @@
     bands, planes, rows, cols = orbitals.shape
     depth = planes * ng
     lines = rows // ng
-    lag = 3
+    lag, delay = 4, 3
     dma = pltpu.SemaphoreType.DMA
     one = (planes, rows, cols)
     two = (planes, 2, rows, cols)
     return pl.pallas_call(
-        functools.partial(field_kernel, ng, nb, lag),
+        functools.partial(field_kernel, ng, nb, lag, delay),
         name="fields",
         out_shape=(
             jax.ShapeDtypeStruct((2, planes, rows, cols), f32),

time: 39.2 us -> 37.7 us (0.962)
  Pallas kernels: 36.7 us -> 35.2 us
    pallas_call x1, Pallas kernels: 36.7 us -> 35.2 us  [fast(): pl.pallas_call(functools.partial(field_kernel, ng, nb, lag, delay), name=...]
where the time goes in v3:
time: 37.7 us; the launch traced here: 37.6 us
  Pallas kernels  35.2 us (93%)
  local copies, waits for them, and re-layouts  1.77 us (5%)
  between operations  0.64 us (2%)
    pallas_call x1, Pallas kernels, fast(): pl.pallas_call(functools.partial(field_kernel, ng, nb, lag, delay), name=...  35.2 us
    unnamed x2, local copies, waits for them, and re-layouts  1.77 us

profile of v3, /device:TPU:0, one launch (start us, length us, event | category | flops | bytes accessed | tf_op | source)
XLA Modules:
  0.0 37.6 jit_solution(218367891553571287)
XLA Ops:
  0.6 35.2 %fields.1 = (f32[2,8,64,128]{3,2,1,0:T(8,128)S(1)}, bf16[8,8,64,128]{3,2,1,0:T(8,128)(2,1)S(1)}) custom-call(s32[8]{0:T(128)} %occ_hbm.1, s32[8]{0:T(128)} %spin_hbm.1, bf16[8,8,64,128]{3,2,1,0:T(8,128)(2,1)} %orb_hbm.1, f32[8,64,128]{2,1,0:T(8,128)} %ion_hbm.1, bf16[384,128]{1,0:T(8,128)(2,1)} %constant.4.clone.hx_hbm, ...), custom_call_target="tpu_custom_call" | custom-call | tf_op jit(solution)/shard_map/fields/pallas_call | solution.py:435
  35.8 0.8 %copy.11 = f32[2,8,64,128]{3,2,1,0:T(8,128)} copy(f32[2,8,64,128]{3,2,1,0:T(8,128)S(1)} %get-tuple-element.4) | data formatting | bytes 1048576
  36.6 1.0 %copy.12 = bf16[8,8,64,128]{3,2,1,0:T(8,128)(2,1)} copy(bf16[8,8,64,128]{3,2,1,0:T(8,128)(2,1)S(1)} %get-tuple-element.5) | data formatting | bytes 2097152
